TPU v7x, 256 devices: a whole 4x4x8 slice. The times are simulated.
256 devices in a mesh: kvp: 32 (over z, x), head: 8 (over y, core).
Axes of the slice: x: 4, y: 4, z: 8, core: 2. Of those that a mesh axis runs over, the one named last changes fastest.
Arguments:
- hidden_in: bfloat16 [16, 8192], P(None, 'kvp'), may hold values from -4 to 4
- attn_gain: bfloat16 [8192], P('kvp'), may hold values from 0.25 to 1.75
- query_key_value_weight: bfloat16 [8192, 8, 1280], P('kvp', 'head'), may hold values from -0.0625 to 0.0625
- k_cache: bfloat16 [8, 2048, 128, 128], P('head', 'kvp'), may hold values from -1200 to 1200
- value_cache: bfloat16 [8, 2048, 128, 128], P('head', 'kvp'), may hold values from -48 to 48
- page_table: int32 [16, 128], P(None, 'kvp'), may hold values from 0 to 63, as said below
- lengths: int32 [16], replicated, may hold values from 4096 to 16384, as said below
- output_weight: bfloat16 [8, 1024, 8192], P('head', None, 'kvp'), may hold values from -0.1875 to 0.1875
- mlp_gain: bfloat16 [8192], P('kvp'), may hold values from 0.099609375 to 1.8984375
- w_in: bfloat16 [8192, 2, 22016], P('kvp', None, 'head'), may hold values from -0.0625 to 0.0625
- w_down: bfloat16 [22016, 8192], P('head', 'kvp'), may hold values from -0.15625 to 0.15625
Outputs:
- next_hidden: bfloat16 [16, 8192], P(None, 'kvp')
Inputs may be any that keep to these rules, and one draw needn't show every extreme that they name: `page_table`: within each aligned block of 4 columns, the 16 x 4 entries are a permutation of 0 to 63. `lengths`: in every draw some request has exactly 16384 cached tokens.
All inputs are finite; a program needn't handle non-finite values.
Results may differ from a plain program's by a relative error of at most 0.033.
Values may be sent and summed in bfloat16 or wider, within the bound.
A program may use at most 64 MiB of HBM per device.

v0:
```python
import functools
import math

import jax
import jax.numpy as jnp
import numpy as np
from jax import lax
from jax.experimental import pallas as pl
from jax.experimental.pallas import tpu as pltpu
from jax.sharding import PartitionSpec as P

MESH = pl.DeviceIdType.MESH
F32 = jnp.float32
BF16 = jnp.bfloat16

MODEL_WIDTH = 8192
EPSILON = 1e-05
ROPE_BASE = 10000.0
B = 16
G = 8
D = 128
Z, X = 8, 4
N = Z * X
Y, C = 4, 2
H = Y * C
PAGE = 128
PAGES_HERE = 4
VECTORS = G + 2
LANES = 128
TURNS = 8
TILE = 120
SQUARE_ROW = VECTORS
GROUPS = (4, 6, 6, 6)
OWNERS = 16
SUMMING = 1
SPREAD, UNSPREAD = 5, 13


def around(offset, size):
    return min(offset % size, -offset % size)


def far_first(offsets, sizes):
    return sorted(offsets, key=lambda at: -sum(around(o, s) for o, s in zip(at, sizes)))


ALL = far_first([(dz, dx) for dz in range(Z) for dx in range(X) if (dz, dx) != (0, 0)], (Z, X))
NEAR = far_first(
    [(dz, dx) for dz in (-1, 0, 1, 2) for dx in range(X) if (dz, dx) != (0, 0)], (Z, X)
)
HEADS = far_first([(dy, dc) for dy in range(Y) for dc in range(C) if (dy, dc) != (0, 0)], (Y, C))


ROWS = OWNERS // X
NEAREST_ROWS = [sorted(range(ROWS), key=lambda row: around(row - z, Z)) for z in range(Z)]


def iota(shape, dim):
    return lax.broadcasted_iota(jnp.int32, shape, dim)


def rounded(value):
    return value.astype(BF16).astype(F32)


def sine_and_cosine(angle):
    turns = jnp.floor(angle * (1.0 / (2.0 * math.pi)) + 0.5)
    left = angle - turns * 6.28125
    left = left - turns * (2.0 * math.pi - 6.28125)
    y = left * 0.5
    z = y * y
    sine, cosine = 0.0, 0.0
    for k in range(6, -1, -1):
        sine = sine * z + (-1.0) ** k / math.factorial(2 * k + 1)
    sine = sine * y
    for k in range(7, -1, -1):
        cosine = cosine * z + (-1.0) ** k / math.factorial(2 * k)
    return 2.0 * sine * cosine, 1.0 - 2.0 * sine * sine


def kernel(
    tiles_ff,
    ff,
    hidden_hbm,
    attn_gain_hbm,
    qkv_hbm,
    k_hbm,
    v_hbm,
    table_hbm,
    lengths_hbm,
    wo_hbm,
    mlp_gain_hbm,
    win_hbm,
    wdown_hbm,
    inverse_hbm,
    out_ref,
    hidden,
    attn_gain,
    mlp_gain,
    inverse,
    table,
    lengths,
    wqkv,
    keys,
    values,
    keys_across,
    wo,
    win,
    win_across,
    wdown,
    turned,
    qkv_send,
    qkv_recv,
    q_all,
    tile,
    part_send,
    part_recv,
    joined,
    attn_all,
    attn_rows,
    head_send,
    head_recv,
    ff_send,
    ff_recv,
    units,
    hid_all,
    last_send,
    last_recv,
    owners,
    tiles,
    local_sem,
    query_sem,
    sum_sem,
    tile_sem,
    all_sem,
    send_sem,
    recv_sem,
):
    me = lax.axis_index("kvp")
    my_head = lax.axis_index("head")
    my_z, my_x = me // X, lax.rem(me, X)
    my_y, my_c = my_head // C, lax.rem(my_head, C)
    zs = [lax.rem(my_z + dz, Z) for dz in range(Z)]
    xs = [lax.rem(my_x + dx, X) for dx in range(X)]
    ys = [lax.rem(my_y + dy, Y) for dy in range(Y)]
    cs = [lax.rem(my_c + dc, C) for dc in range(C)]

    sums = my_c == SUMMING

    def at(kvp, plane):
        return {"kvp": kvp, "head": my_y * C + plane}

    def kvp_at(dz, dx):
        return zs[dz % Z] * X + xs[dx % X]

    def head_peer(dy, dc):
        return {"head": ys[dy] * C + cs[dc]}

    request_of_z = [lax.rem(z, Z // 2) * X for z in zs]

    def request_at(dz, dx):
        return request_of_z[dz % Z] + xs[dx % X]

    my_request = request_at(0, 0)
    my_tile = lax.rem(me * UNSPREAD, N)

    def copy_to(src, dst, phase, device, arrival=None):
        pltpu.make_async_remote_copy(
            src_ref=src,
            dst_ref=dst,
            send_sem=send_sem.at[phase],
            recv_sem=recv_sem.at[phase] if arrival is None else arrival,
            device_id=device,
            device_id_type=MESH,
        ).start()

    def waiter(ref, phase, arrival=None):
        return pltpu.make_async_remote_copy(
            src_ref=ref,
            dst_ref=ref,
            send_sem=send_sem.at[phase],
            recv_sem=recv_sem.at[phase] if arrival is None else arrival,
            device_id={"kvp": kvp_at(1, 0)},
            device_id_type=MESH,
        )

    pairs = [
        (hidden_hbm, hidden),
        (attn_gain_hbm, attn_gain),
        (qkv_hbm, wqkv),
        (lengths_hbm, lengths),
        (inverse_hbm, inverse),
        (table_hbm, table),
        (k_hbm.at[pl.ds(0, 32)], keys.at[pl.ds(0, 32)]),
        (k_hbm.at[pl.ds(32, 32)], keys.at[pl.ds(32, 32)]),
        (v_hbm.at[pl.ds(0, 32)], values.at[pl.ds(0, 32)]),
        (v_hbm.at[pl.ds(32, 32)], values.at[pl.ds(32, 32)]),
        (wo_hbm, wo),
        (mlp_gain_hbm, mlp_gain),
        (win_hbm.at[0], win.at[0, pl.ds(0, ff)]),
        (win_hbm.at[1], win.at[1, pl.ds(0, ff)]),
        (wdown_hbm, wdown.at[pl.ds(0, ff)]),
    ]
    copies = [
        pltpu.make_async_copy(src, dst, local_sem.at[at]) for at, (src, dst) in enumerate(pairs)
    ]
    for copy in copies[:3]:
        copy.start()
    barrier = pltpu.get_barrier_semaphore()

    @pl.when(sums & (me < OWNERS))
    def _():
        for offset in ALL:
            for plane in range(C):
                pl.semaphore_signal(
                    barrier, inc=1, device_id=at(kvp_at(*offset), plane), device_id_type=MESH
                )
        pl.semaphore_signal(barrier, inc=1, device_id=at(me, 0), device_id_type=MESH)

    for offset in HEADS:
        pl.semaphore_signal(barrier, inc=1, device_id=head_peer(*offset), device_id_type=MESH)
    for copy in copies[3:]:
        copy.start()

    count, count_ff = 0, 0
    for offset in ALL:
        device = kvp_at(*offset)
        owners[count] = device
        count = count + jnp.where(device < OWNERS, 1, 0)
        candidate = lax.rem(device * UNSPREAD, N)
        tiles[count_ff] = candidate
        count_ff = count_ff + jnp.where(candidate < tiles_ff, 1, 0)

    @pl.when(me < OWNERS)
    def _():
        owners[OWNERS - 1] = me

    @pl.when(my_tile < tiles_ff)
    def _():
        tiles[tiles_ff - 1] = my_tile

    pad = win.shape[1] - ff
    win[:, pl.ds(ff, pad), :] = jnp.zeros((2, pad, win.shape[2]), BF16)
    wdown[pl.ds(ff, pad), :] = jnp.zeros((pad, wdown.shape[1]), BF16)
    turned[...] = jnp.zeros(turned.shape, F32)

    for copy in copies[:3]:
        copy.wait()
    x = hidden[...].astype(F32)
    normed = (x * attn_gain[...][None, :].astype(F32)).astype(BF16)
    partial = jnp.dot(normed, wqkv[...], preferred_element_type=F32)
    for v in range(VECTORS):
        turned[pl.ds(v, B, stride=2 * G), :] = partial[:, v * D : (v + 1) * D]
    square = jnp.sum(x * x, axis=1, keepdims=True)
    high = rounded(square)
    turned[pl.ds(SQUARE_ROW, B, stride=2 * G), :] = jnp.where(
        iota((B, LANES), 1) < LANES // 2, high, square - high
    )
    qkv_send[...] = turned[...].reshape(B, 2 * G, D).astype(BF16)
    pl.semaphore_wait(
        barrier, jnp.where(sums & (me < OWNERS), OWNERS - 1, OWNERS) + len(HEADS)
    )

    def send_qkv(step):
        owner = owners[step]
        copy_to(
            qkv_send.at[owner],
            qkv_recv.at[my_c, me],
            0,
            at(owner, SUMMING),
            sum_sem.at[0, my_c],
        )

    for step in range(OWNERS - 1):
        send_qkv(step)

    @pl.when((me >= OWNERS) | (my_c != SUMMING))
    def _():
        send_qkv(OWNERS - 1)

    for copy in copies[3:6]:
        copy.wait()
    sine, cosine = sine_and_cosine(lengths[my_request].astype(F32) * inverse[...])
    lane = iota((G, LANES), 1)
    sine = jnp.where(lane < D // 2, -sine, sine)[0:1]
    cosine = cosine[0:1]
    for copy in copies[6:10]:
        copy.wait()

    @pl.loop(0, keys.shape[0] // TURNS)
    def _(step):
        for turn in range(TURNS):
            keys_across[step * TURNS + turn] = keys[step * TURNS + turn].T

    for copy in copies[11:14]:
        copy.wait()
    for t in range(tiles_ff):
        for part in range(2):
            win_across[t, part] = win[part, pl.ds(t * TILE, LANES), :].T


    def wait_parts(recv_ref, phase, plane):
        arrived = recv_ref.at[plane] if plane != SUMMING else recv_ref.at[plane, pl.ds(0, N - 1)]
        waiter(arrived, 0, sum_sem.at[phase, plane]).wait_recv()

    @pl.when(sums & (me < OWNERS))
    def _():
        qkv_recv[SUMMING, me] = qkv_send[my_request]
        for plane in (SUMMING, 1 - SUMMING):
            wait_parts(qkv_recv, 0, plane)
            total = jnp.sum(qkv_recv[plane].astype(F32), axis=0)
            square = total[SQUARE_ROW : SQUARE_ROW + 1]
            square = square[:, 0:1] + square[:, LANES // 2 : LANES // 2 + 1]
            total = total * lax.rsqrt(square / MODEL_WIDTH + EPSILON)
            rotated = total * cosine + pltpu.roll(total, D // 2, 1) * sine
            tile[plane] = jnp.where(iota((2 * G, LANES), 0) <= G, rotated, total).astype(BF16)
            for offset in ALL + [(0, 0)]:
                if offset != (0, 0) or plane != SUMMING:
                    copy_to(
                        tile.at[plane, pl.ds(0, G)],
                        q_all.at[me],
                        1 + plane,
                        at(kvp_at(*offset), plane),
                        query_sem.at[my_z],
                    )
            copy_to(
                tile.at[plane],
                tile.at[plane],
                3 + plane,
                at(kvp_at(Z // 2, 0), SUMMING),
                tile_sem.at[plane],
            )
        q_all[me] = tile[SUMMING, pl.ds(0, G)]

    factor = D ** (-0.5)
    first = me * (PAGES_HERE * PAGE)

    def attend(requests):
        slots = [[table[p, b] for p in range(PAGES_HERE)] for b in requests]
        queries = [q_all[b] for b in requests]
        scores = [
            [
                jnp.dot(query, keys_across[slot], preferred_element_type=F32)
                for slot in here
            ]
            for query, here in zip(queries, slots)
        ]
        parts = []
        for b, here, products in zip(requests, slots, scores):
            left = lengths[b] - first
            live = [lane + p * PAGE < left for p in range(PAGES_HERE)]
            masked = [jnp.where(ok, s * factor, -1e30) for ok, s in zip(live, products)]
            top = jnp.max(functools.reduce(jnp.maximum, masked), axis=1, keepdims=True)
            weights = [jnp.where(ok, jnp.exp(s - top), 0.0) for ok, s in zip(live, masked)]
            total = jnp.sum(functools.reduce(jnp.add, weights), axis=1, keepdims=True)
            summed = 0.0
            for p in range(PAGES_HERE):
                summed = summed + jnp.dot(
                    weights[p].astype(BF16), values[here[p]], preferred_element_type=F32
                )
            high = rounded(top)
            middle = rounded(top - high)
            low = top - high - middle
            stats = jnp.where(
                lane < 32, high, jnp.where(lane < 64, middle, jnp.where(lane < 96, low, total))
            )
            parts.append(jnp.concatenate([summed, stats], axis=0).astype(BF16))
        for b, part in zip(requests, parts):
            part_send[b] = part

    def send_part(request, target):
        copy_to(
            part_send.at[request],
            part_recv.at[my_c, me],
            5,
            at(target, SUMMING),
            sum_sem.at[1, my_c],
        )

    for place in range(ROWS):
        row = 0
        for z in range(Z):
            row = jnp.where(my_z == z, NEAREST_ROWS[z][place], row)
        requests = [row * X + x for x in range(X)]
        if place == 0:

            @pl.when(sums & (me < OWNERS))
            def _(row=row):
                waiter(q_all.at[pl.ds(0, X - 1)], 0, query_sem.at[row]).wait_recv()

            @pl.when(jnp.logical_not(sums & (me < OWNERS)))
            def _(row=row):
                waiter(q_all.at[pl.ds(0, X)], 0, query_sem.at[row]).wait_recv()

        else:
            waiter(q_all.at[pl.ds(0, X)], 0, query_sem.at[row]).wait_recv()
        attend(requests)
        for request in requests:
            for target in (request + OWNERS, request):

                @pl.when((me != target) | (my_c != SUMMING))
                def _(request=request, target=target):
                    send_part(request, target)

    copies[10].wait()

    @pl.when(sums)
    def _():
        part_recv[SUMMING, me] = part_send[my_request]
        for plane in (SUMMING, 1 - SUMMING):

            @pl.when(me >= OWNERS)
            def _(plane=plane):
                waiter(tile.at[plane], 0, tile_sem.at[plane]).wait_recv()

            known = tile[plane].astype(F32)
            new_key, new_value = known[G : G + 1], known[G + 1 : G + 2]
            own = jnp.sum(known[:G] * new_key, axis=1, keepdims=True) * factor
            wait_parts(part_recv, 1, plane)
            tops, overall = [], own
            for k in range(N):
                stats = part_recv[plane, k].astype(F32)[G:]
                tops.append(stats[:, 0:1] + stats[:, 32:33] + stats[:, 64:65])
                overall = jnp.maximum(overall, tops[k])
            own_weight = jnp.exp(own - overall)
            total = own_weight
            summed = rounded(own_weight) * new_value
            for k in range(N):
                part = part_recv[plane, k].astype(F32)
                carried = jnp.exp(tops[k] - overall)
                total = total + part[G:, 96:97] * carried
                summed = summed + part[:G] * carried
            joined[plane] = (summed / total).astype(BF16)
            for offset in NEAR + [(0, 0)]:
                if offset != (0, 0) or plane != SUMMING:
                    copy_to(
                        joined.at[plane],
                        attn_all.at[my_request],
                        6 + plane,
                        at(kvp_at(*offset), plane),
                        all_sem.at[0],
                    )
        attn_all[my_request] = joined[SUMMING]
        waiter(attn_all.at[pl.ds(0, len(NEAR))], 0, all_sem.at[0]).wait_recv()

    @pl.when(my_c != SUMMING)
    def _():
        waiter(attn_all, 0, all_sem.at[0]).wait_recv()

    attn_rows[...] = attn_all[...].astype(F32).reshape(B * G, D)
    attn = jnp.concatenate(
        [attn_rows[pl.ds(g, B, stride=G), :].astype(BF16) for g in range(G)], axis=1
    )

    def over_heads(term, send_ref, recv_ref, phase):
        send_ref[...] = term.astype(BF16)
        for offset in HEADS:
            copy_to(send_ref, recv_ref.at[my_head], phase, head_peer(*offset))
        recv_ref[my_head] = term.astype(BF16)
        waiter(recv_ref.at[pl.ds(0, len(HEADS))], phase).wait_recv()
        return jnp.sum(recv_ref[...].astype(F32), axis=0)

    term = jnp.dot(attn, wo[...], preferred_element_type=F32)
    stream = x + over_heads(term, head_send, head_recv, 8)

    square = jnp.sum(stream * stream, axis=1, keepdims=True)
    high = rounded(square)
    column = iota((B, LANES), 1)
    normed = (stream * mlp_gain[...][None, :].astype(F32)).astype(BF16)
    ours = [tiles[step] for step in range(tiles_ff)]

    def make(step):
        for part in range(2):
            product = jnp.dot(normed, win_across[ours[step], part], preferred_element_type=F32)
            rest = jnp.where(column == TILE, high, square - high) if part == 0 else 0.0
            ff_send[ours[step], part] = jnp.where(column < TILE, product, rest).astype(BF16)

    def send(step):
        copy_to(
            ff_send.at[ours[step]],
            ff_recv.at[my_c, me],
            10,
            at(lax.rem(ours[step] * SPREAD, N), SUMMING),
            sum_sem.at[2, my_c],
        )

    start = 0
    for size in GROUPS:
        for step in range(start, start + size):
            make(step)
        for step in range(start, start + size):
            send(step)
        start += size
    make(start)

    @pl.when((my_tile >= tiles_ff) | (my_c != SUMMING))
    def _():
        send(start)

    summing_tile = sums & (my_tile < tiles_ff)

    @pl.when(summing_tile)
    def _():
        ff_recv[SUMMING, me] = ff_send[my_tile]
        for plane in (SUMMING, 1 - SUMMING):
            wait_parts(ff_recv, 2, plane)
            both = jnp.sum(ff_recv[plane].astype(F32), axis=0)
            square = both[0][:, TILE : TILE + 1] + both[0][:, TILE + 1 : TILE + 2]
            scale = lax.rsqrt(square / MODEL_WIDTH + EPSILON)
            gate, up = both[0] * scale, both[1] * scale
            active = gate / (1.0 + jnp.exp(-gate)) * up
            units[plane] = jnp.where(column < TILE, active, 0.0).astype(BF16)
            for offset in ALL + [(0, 0)]:
                if offset != (0, 0) or plane != SUMMING:
                    copy_to(
                        units.at[plane],
                        hid_all.at[my_tile],
                        11 + plane,
                        at(kvp_at(*offset), plane),
                        all_sem.at[1],
                    )
        hid_all[my_tile] = units[SUMMING]
        waiter(hid_all.at[pl.ds(0, tiles_ff - 1)], 0, all_sem.at[1]).wait_recv()

    @pl.when(jnp.logical_not(summing_tile))
    def _():
        waiter(hid_all, 0, all_sem.at[1]).wait_recv()

    copies[14].wait()
    term = 0.0
    for t in range(tiles_ff):
        term = term + jnp.dot(
            hid_all[t], wdown[pl.ds(t * TILE, LANES), :], preferred_element_type=F32
        )
    out_ref[...] = (stream + over_heads(term, last_send, last_recv, 9)).astype(BF16)

    @pl.when(sums & (me < OWNERS))
    def _():
        waiter(qkv_recv.at[0, pl.ds(0, OWNERS - 1)], 0).wait_send()
        for plane in range(C):
            count = N if plane != SUMMING else N - 1
            waiter(qkv_recv.at[0, pl.ds(0, count), pl.ds(0, G)], 1 + plane).wait_send()
            waiter(tile.at[plane], 3 + plane).wait_send()

    @pl.when(jnp.logical_not(sums & (me < OWNERS)))
    def _():
        waiter(qkv_recv.at[0, pl.ds(0, OWNERS)], 0).wait_send()

    @pl.when(sums)
    def _():
        waiter(part_recv.at[0, pl.ds(0, N - 1)], 5).wait_send()
        for plane in range(C):
            count = len(NEAR) + (plane != SUMMING)
            waiter(attn_all.at[pl.ds(0, count)], 6 + plane).wait_send()

    @pl.when(my_c != SUMMING)
    def _():
        waiter(part_recv.at[0], 5).wait_send()

    waiter(head_recv.at[pl.ds(0, len(HEADS))], 8).wait_send()
    waiter(last_recv.at[pl.ds(0, len(HEADS))], 9).wait_send()

    @pl.when(summing_tile)
    def _():
        waiter(ff_recv.at[0, pl.ds(0, tiles_ff - 1)], 10).wait_send()
        for plane in range(C):
            count = N if plane != SUMMING else N - 1
            waiter(part_recv.at[0, pl.ds(0, count)], 11 + plane).wait_send()

    @pl.when(jnp.logical_not(summing_tile))
    def _():
        waiter(ff_recv.at[0, pl.ds(0, tiles_ff)], 10).wait_send()


def on_device(
    hidden_in,
    attn_gain,
    query_key_value_weight,
    k_cache,
    value_cache,
    page_table,
    lengths,
    output_weight,
    mlp_gain,
    w_in,
    w_down,
):
    width = hidden_in.shape[1]
    ff = w_down.shape[0]
    tiles_ff = -(-ff // TILE)
    half = D // 2
    inverse = ROPE_BASE ** (-np.arange(half, dtype=np.float64) * (2.0 / D))
    inverse = np.broadcast_to(np.concatenate([inverse, inverse]), (8, D)).astype(np.float32)
    slots = k_cache.shape[1]
    return pl.pallas_call(
        functools.partial(kernel, tiles_ff, ff),
        out_shape=pltpu.VMEM((B, width), BF16),
        in_specs=[pl.BlockSpec(memory_space=pl.ANY)] * 12,
        out_specs=pl.BlockSpec(memory_space=pltpu.VMEM),
        scratch_shapes=[
            pltpu.VMEM((B, width), BF16),
            pltpu.VMEM((width,), BF16),
            pltpu.VMEM((width,), BF16),
            pltpu.VMEM((8, D), F32),
            pltpu.SMEM((PAGES_HERE, B), jnp.int32),
            pltpu.SMEM((B,), jnp.int32),
            pltpu.VMEM((width, VECTORS * D), BF16),
            pltpu.VMEM((slots, PAGE, D), BF16),
            pltpu.VMEM((slots, PAGE, D), BF16),
            pltpu.VMEM((slots, D, PAGE), BF16),
            pltpu.VMEM((G * D, width), BF16),
            pltpu.VMEM((2, (tiles_ff - 1) * TILE + LANES, width), BF16),
            pltpu.VMEM((tiles_ff, 2, width, LANES), BF16),
            pltpu.VMEM(((tiles_ff - 1) * TILE + LANES, width), BF16),
            pltpu.VMEM((B * 2 * G, D), F32),
            pltpu.VMEM((B, 2 * G, D), BF16),
            pltpu.VMEM((C, N, 2 * G, D), BF16),
            pltpu.VMEM((B, G, D), BF16),
            pltpu.VMEM((C, 2 * G, D), BF16),
            pltpu.VMEM((B, 2 * G, D), BF16),
            pltpu.VMEM((C, N, 2 * G, D), BF16),
            pltpu.VMEM((C, G, D), BF16),
            pltpu.VMEM((B, G, D), BF16),
            pltpu.VMEM((B * G, D), F32),
            pltpu.VMEM((B, width), BF16),
            pltpu.VMEM((H, B, width), BF16),
            pltpu.VMEM((tiles_ff, 2, B, LANES), BF16),
            pltpu.VMEM((C, N, 2, B, LANES), BF16),
            pltpu.VMEM((C, B, LANES), BF16),
            pltpu.VMEM((tiles_ff, B, LANES), BF16),
            pltpu.VMEM((B, width), BF16),
            pltpu.VMEM((H, B, width), BF16),
            pltpu.SMEM((N,), jnp.int32),
            pltpu.SMEM((N,), jnp.int32),
            pltpu.SemaphoreType.DMA((15,)),
            pltpu.SemaphoreType.DMA((ROWS,)),
            pltpu.SemaphoreType.DMA((3, C)),
            pltpu.SemaphoreType.DMA((C,)),
            pltpu.SemaphoreType.DMA((2,)),
            pltpu.SemaphoreType.DMA((13,)),
            pltpu.SemaphoreType.DMA((13,)),
        ],
        compiler_params=pltpu.CompilerParams(collective_id=0, has_side_effects=True),
    )(
        hidden_in,
        attn_gain,
        query_key_value_weight.transpose(1, 0, 2)[0],
        k_cache[0],
        value_cache[0],
        page_table.T,
        lengths,
        output_weight[0],
        mlp_gain,
        w_in.transpose(1, 2, 0),
        w_down,
        jnp.asarray(inverse),
    )


def solution(mesh):
    return jax.shard_map(
        on_device,
        mesh=mesh,
        in_specs=(
            P(None, "kvp"),
            P("kvp"),
            P("kvp", "head", None),
            P("head", "kvp", None, None),
            P("head", "kvp", None, None),
            P(None, "kvp"),
            P(),
            P("head", None, "kvp"),
            P("kvp"),
            P("kvp", None, "head"),
            P("head", "kvp"),
        ),
        out_specs=P(None, "kvp"),
        check_vma=False,
    )
```

profile of v0, /device:TPU:1, one launch (start us, length us, event | category | flops | bytes accessed | tf_op | source)
XLA Modules:
  0.0 54.3 jit_solution(461713658876628485)
XLA Ops:
  0.0 53.7 %shard_map.118 = bf16[16,256]{1,0:T(8,128)(2,1)S(1)} custom-call(bf16[16,256]{1,0:T(8,128)(2,1)} %hidden_hbm.1, bf16[256]{0:T(256)(128)(2,1)} %attn_gain_hbm.1, bf16[256,1280]{1,0:T(8,128)(2,1)} %bitcast.9, bf16[64,128,128]{2,1,0:T(8,128)(2,1)} %bitcast.7, bf16[64,128,128]{2,1,0:T(8,128)(2,1)} %bitcast.8, s32[4,16]{1,0:T(4,128)} %bitcast.11, s32[16]{0:T(128)} %lengths_hbm.1, ...), custom_call_target="tpu_custom_call" | custom-call | tf_op jit(solution)/shard_map/pallas_call | solution.py:595
  53.7 0.6 %copy.14 = bf16[16,256]{1,0:T(8,128)(2,1)} copy(bf16[16,256]{1,0:T(8,128)(2,1)S(1)} %shard_map.118) | data formatting | bytes 16384
where the time goes:
time: 54.4 us; the launch traced here: 54.3 us
  Pallas kernels  53.7 us (99%)
  local copies, waits for them, and re-layouts  0.6 us (1%)
    pallas_call x1, Pallas kernels, on_device(): pl.pallas_call(functools.partial(kernel, tiles_ff, ff), out_shape=pltpu.V...  53.7 us

commit v1 on v0

--- a/solution.py
+++ b/solution.py
@@ -30,6 +30,7 @@
 TURNS = 8
 TILE = 120
 SQUARE_ROW = VECTORS
+REST = 4
 GROUPS = (4, 6, 6, 6)
 OWNERS = 16
 SUMMING = 1
@@ -111,6 +112,8 @@
     turned,
     qkv_send,
     qkv_recv,
+    rest_send,
+    rest_recv,
     q_all,
     tile,
     part_send,
@@ -256,7 +259,9 @@
     turned[pl.ds(SQUARE_ROW, B, stride=2 * G), :] = jnp.where(
         iota((B, LANES), 1) < LANES // 2, high, square - high
     )
-    qkv_send[...] = turned[...].reshape(B, 2 * G, D).astype(BF16)
+    wide = turned[...].reshape(B, 2 * G, D)
+    qkv_send[...] = wide[:, :G].astype(BF16)
+    rest_send[...] = wide[:, G : G + REST].astype(BF16)
     pl.semaphore_wait(
         barrier, jnp.where(sums & (me < OWNERS), OWNERS - 1, OWNERS) + len(HEADS)
     )
@@ -270,6 +275,13 @@
             at(owner, SUMMING),
             sum_sem.at[0, my_c],
         )
+        copy_to(
+            rest_send.at[owner],
+            rest_recv.at[my_c, me],
+            13,
+            at(owner, SUMMING),
+            sum_sem.at[3, my_c],
+        )
 
     for step in range(OWNERS - 1):
         send_qkv(step)
@@ -306,12 +318,16 @@
     @pl.when(sums & (me < OWNERS))
     def _():
         qkv_recv[SUMMING, me] = qkv_send[my_request]
+        rest_recv[SUMMING, me] = rest_send[my_request]
         for plane in (SUMMING, 1 - SUMMING):
+            wait_parts(rest_recv, 3, plane)
+            rest = jnp.sum(rest_recv[plane].astype(F32), axis=0)
+            square = rest[SQUARE_ROW - G : SQUARE_ROW - G + 1]
+            square = square[:, 0:1] + square[:, LANES // 2 : LANES // 2 + 1]
+            scale = lax.rsqrt(square / MODEL_WIDTH + EPSILON)
             wait_parts(qkv_recv, 0, plane)
             total = jnp.sum(qkv_recv[plane].astype(F32), axis=0)
-            square = total[SQUARE_ROW : SQUARE_ROW + 1]
-            square = square[:, 0:1] + square[:, LANES // 2 : LANES // 2 + 1]
-            total = total * lax.rsqrt(square / MODEL_WIDTH + EPSILON)
+            total = jnp.concatenate([total, rest, jnp.zeros_like(rest)], axis=0) * scale
             rotated = total * cosine + pltpu.roll(total, D // 2, 1) * sine
             tile[plane] = jnp.where(iota((2 * G, LANES), 0) <= G, rotated, total).astype(BF16)
             for offset in ALL + [(0, 0)]:
@@ -537,14 +553,16 @@
     @pl.when(sums & (me < OWNERS))
     def _():
         waiter(qkv_recv.at[0, pl.ds(0, OWNERS - 1)], 0).wait_send()
+        waiter(rest_recv.at[0, pl.ds(0, OWNERS - 1)], 13).wait_send()
         for plane in range(C):
             count = N if plane != SUMMING else N - 1
-            waiter(qkv_recv.at[0, pl.ds(0, count), pl.ds(0, G)], 1 + plane).wait_send()
+            waiter(qkv_recv.at[0, pl.ds(0, count)], 1 + plane).wait_send()
             waiter(tile.at[plane], 3 + plane).wait_send()
 
     @pl.when(jnp.logical_not(sums & (me < OWNERS)))
     def _():
         waiter(qkv_recv.at[0, pl.ds(0, OWNERS)], 0).wait_send()
+        waiter(rest_recv.at[0, pl.ds(0, OWNERS)], 13).wait_send()
 
     @pl.when(sums)
     def _():
@@ -613,8 +631,10 @@
             pltpu.VMEM((tiles_ff, 2, width, LANES), BF16),
             pltpu.VMEM(((tiles_ff - 1) * TILE + LANES, width), BF16),
             pltpu.VMEM((B * 2 * G, D), F32),
-            pltpu.VMEM((B, 2 * G, D), BF16),
-            pltpu.VMEM((C, N, 2 * G, D), BF16),
+            pltpu.VMEM((B, G, D), BF16),
+            pltpu.VMEM((C, N, G, D), BF16),
+            pltpu.VMEM((B, REST, D), BF16),
+            pltpu.VMEM((C, N, REST, D), BF16),
             pltpu.VMEM((B, G, D), BF16),
             pltpu.VMEM((C, 2 * G, D), BF16),
             pltpu.VMEM((B, 2 * G, D), BF16),
@@ -634,11 +654,11 @@
             pltpu.SMEM((N,), jnp.int32),
             pltpu.SemaphoreType.DMA((15,)),
             pltpu.SemaphoreType.DMA((ROWS,)),
-            pltpu.SemaphoreType.DMA((3, C)),
+            pltpu.SemaphoreType.DMA((4, C)),
             pltpu.SemaphoreType.DMA((C,)),
             pltpu.SemaphoreType.DMA((2,)),
-            pltpu.SemaphoreType.DMA((13,)),
-            pltpu.SemaphoreType.DMA((13,)),
+            pltpu.SemaphoreType.DMA((14,)),
+            pltpu.SemaphoreType.DMA((14,)),
         ],
         compiler_params=pltpu.CompilerParams(collective_id=0, has_side_effects=True),
     )(

time: 54.4 us -> 54 us (level)
  no operation moved by 1% of the time
where the time goes in v1:
time: 54 us; the launch traced here: 53.9 us
  Pallas kernels  53.3 us (99%)
  local copies, waits for them, and re-layouts  0.6 us (1%)
    pallas_call x1, Pallas kernels, on_device(): pl.pallas_call(functools.partial(kernel, tiles_ff, ff), out_shape=pltpu.V...  53.3 us

profile of v1, /device:TPU:1, one launch (start us, length us, event | category | flops | bytes accessed | tf_op | source)
XLA Modules:
  0.0 53.9 jit_solution(18122968585395400044)
XLA Ops:
  0.0 53.3 %shard_map.118 = bf16[16,256]{1,0:T(8,128)(2,1)S(1)} custom-call(bf16[16,256]{1,0:T(8,128)(2,1)} %hidden_hbm.1, bf16[256]{0:T(256)(128)(2,1)} %attn_gain_hbm.1, bf16[256,1280]{1,0:T(8,128)(2,1)} %bitcast.9, bf16[64,128,128]{2,1,0:T(8,128)(2,1)} %bitcast.7, bf16[64,128,128]{2,1,0:T(8,128)(2,1)} %bitcast.8, s32[4,16]{1,0:T(4,128)} %bitcast.11, s32[16]{0:T(128)} %lengths_hbm.1, ...), custom_call_target="tpu_custom_call" | custom-call | tf_op jit(solution)/shard_map/pallas_call | solution.py:613
  53.3 0.6 %copy.14 = bf16[16,256]{1,0:T(8,128)(2,1)} copy(bf16[16,256]{1,0:T(8,128)(2,1)S(1)} %shard_map.118) | data formatting | bytes 16384

commit v2 on v1

--- a/solution.py
+++ b/solution.py
@@ -30,6 +30,7 @@
 TURNS = 8
 TILE = 120
 SQUARE_ROW = VECTORS
+WIDE = LANES // G
 REST = 4
 GROUPS = (4, 6, 6, 6)
 OWNERS = 16
@@ -115,9 +116,12 @@
     rest_send,
     rest_recv,
     q_all,
+    tile_out,
     tile,
     part_send,
     part_recv,
+    stat_send,
+    stat_recv,
     joined,
     attn_all,
     attn_rows,
@@ -159,12 +163,16 @@
     def head_peer(dy, dc):
         return {"head": ys[dy] * C + cs[dc]}
 
-    request_of_z = [lax.rem(z, Z // 2) * X for z in zs]
+    request_of_z = [lax.rem(z + Z // 4, Z // 2) * X for z in zs]
 
     def request_at(dz, dx):
         return request_of_z[dz % Z] + xs[dx % X]
 
     my_request = request_at(0, 0)
+
+    def joiners(request):
+        return lax.rem(request + 3 * N // 4, N), request + N // 4
+
     my_tile = lax.rem(me * UNSPREAD, N)
 
     def copy_to(src, dst, phase, device, arrival=None):
@@ -292,7 +300,7 @@
 
     for copy in copies[3:6]:
         copy.wait()
-    sine, cosine = sine_and_cosine(lengths[my_request].astype(F32) * inverse[...])
+    sine, cosine = sine_and_cosine(lengths[lax.rem(me, OWNERS)].astype(F32) * inverse[...])
     lane = iota((G, LANES), 1)
     sine = jnp.where(lane < D // 2, -sine, sine)[0:1]
     cosine = cosine[0:1]
@@ -317,8 +325,8 @@
 
     @pl.when(sums & (me < OWNERS))
     def _():
-        qkv_recv[SUMMING, me] = qkv_send[my_request]
-        rest_recv[SUMMING, me] = rest_send[my_request]
+        qkv_recv[SUMMING, me] = qkv_send[me]
+        rest_recv[SUMMING, me] = rest_send[me]
         for plane in (SUMMING, 1 - SUMMING):
             wait_parts(rest_recv, 3, plane)
             rest = jnp.sum(rest_recv[plane].astype(F32), axis=0)
@@ -329,24 +337,31 @@
             total = jnp.sum(qkv_recv[plane].astype(F32), axis=0)
             total = jnp.concatenate([total, rest, jnp.zeros_like(rest)], axis=0) * scale
             rotated = total * cosine + pltpu.roll(total, D // 2, 1) * sine
-            tile[plane] = jnp.where(iota((2 * G, LANES), 0) <= G, rotated, total).astype(BF16)
+            tile_out[plane] = jnp.where(iota((2 * G, LANES), 0) <= G, rotated, total).astype(BF16)
             for offset in ALL + [(0, 0)]:
                 if offset != (0, 0) or plane != SUMMING:
                     copy_to(
-                        tile.at[plane, pl.ds(0, G)],
+                        tile_out.at[plane, pl.ds(0, G)],
                         q_all.at[me],
                         1 + plane,
                         at(kvp_at(*offset), plane),
                         query_sem.at[my_z],
                     )
-            copy_to(
-                tile.at[plane],
-                tile.at[plane],
-                3 + plane,
-                at(kvp_at(Z // 2, 0), SUMMING),
-                tile_sem.at[plane],
-            )
-        q_all[me] = tile[SUMMING, pl.ds(0, G)]
+            for target in joiners(me):
+                copy_to(
+                    tile_out.at[plane],
+                    tile.at[plane],
+                    3 + plane,
+                    at(target, SUMMING),
+                    tile_sem.at[plane],
+                )
+        q_all[me] = tile_out[SUMMING, pl.ds(0, G)]
+
+    head_at = iota((G, LANES), 0) * WIDE
+    in_block = (lane >= head_at) & (lane < head_at + WIDE)
+
+    def to_column(row):
+        return jnp.sum(jnp.where(lane == head_at, row, 0.0), axis=1, keepdims=True)
 
     factor = D ** (-0.5)
     first = me * (PAGES_HERE * PAGE)
@@ -374,15 +389,12 @@
                 summed = summed + jnp.dot(
                     weights[p].astype(BF16), values[here[p]], preferred_element_type=F32
                 )
-            high = rounded(top)
-            middle = rounded(top - high)
-            low = top - high - middle
-            stats = jnp.where(
-                lane < 32, high, jnp.where(lane < 64, middle, jnp.where(lane < 96, low, total))
-            )
-            parts.append(jnp.concatenate([summed, stats], axis=0).astype(BF16))
-        for b, part in zip(requests, parts):
+            both = jnp.where(lane % WIDE < WIDE // 2, top, total)
+            row = jnp.sum(jnp.where(in_block, both, 0.0), axis=0, keepdims=True)
+            parts.append((summed.astype(BF16), row))
+        for b, (part, row) in zip(requests, parts):
             part_send[b] = part
+            stat_send[b] = row
 
     def send_part(request, target):
         copy_to(
@@ -392,6 +404,13 @@
             at(target, SUMMING),
             sum_sem.at[1, my_c],
         )
+        copy_to(
+            stat_send.at[request],
+            stat_recv.at[my_c, pl.ds(me, 1)],
+            14,
+            at(target, SUMMING),
+            sum_sem.at[4, my_c],
+        )
 
     for place in range(ROWS):
         row = 0
@@ -412,7 +431,7 @@
             waiter(q_all.at[pl.ds(0, X)], 0, query_sem.at[row]).wait_recv()
         attend(requests)
         for request in requests:
-            for target in (request + OWNERS, request):
+            for target in joiners(request):
 
                 @pl.when((me != target) | (my_c != SUMMING))
                 def _(request=request, target=target):
@@ -423,29 +442,26 @@
     @pl.when(sums)
     def _():
         part_recv[SUMMING, me] = part_send[my_request]
+        stat_recv[SUMMING, pl.ds(me, 1)] = stat_send[my_request]
         for plane in (SUMMING, 1 - SUMMING):
 
-            @pl.when(me >= OWNERS)
-            def _(plane=plane):
-                waiter(tile.at[plane], 0, tile_sem.at[plane]).wait_recv()
-
+            waiter(tile.at[plane], 0, tile_sem.at[plane]).wait_recv()
             known = tile[plane].astype(F32)
             new_key, new_value = known[G : G + 1], known[G + 1 : G + 2]
             own = jnp.sum(known[:G] * new_key, axis=1, keepdims=True) * factor
+            own_row = jnp.sum(jnp.where(in_block, own, 0.0), axis=0, keepdims=True)
+            wait_parts(stat_recv, 4, plane)
+            stats = stat_recv[plane]
+            overall = jnp.maximum(jnp.max(stats, axis=0, keepdims=True), own_row)
+            carried = jnp.exp(stats - overall)
+            totals = pltpu.roll(stats, LANES - WIDE // 2, 1)
+            own_row = jnp.exp(own_row - overall)
+            total = to_column(jnp.sum(totals * carried, axis=0, keepdims=True) + own_row)
+            summed = rounded(to_column(own_row)) * new_value
+            carried = [to_column(carried[k : k + 1]) for k in range(N)]
             wait_parts(part_recv, 1, plane)
-            tops, overall = [], own
             for k in range(N):
-                stats = part_recv[plane, k].astype(F32)[G:]
-                tops.append(stats[:, 0:1] + stats[:, 32:33] + stats[:, 64:65])
-                overall = jnp.maximum(overall, tops[k])
-            own_weight = jnp.exp(own - overall)
-            total = own_weight
-            summed = rounded(own_weight) * new_value
-            for k in range(N):
-                part = part_recv[plane, k].astype(F32)
-                carried = jnp.exp(tops[k] - overall)
-                total = total + part[G:, 96:97] * carried
-                summed = summed + part[:G] * carried
+                summed = summed + part_recv[plane, k].astype(F32) * carried[k]
             joined[plane] = (summed / total).astype(BF16)
             for offset in NEAR + [(0, 0)]:
                 if offset != (0, 0) or plane != SUMMING:
@@ -557,7 +573,7 @@
         for plane in range(C):
             count = N if plane != SUMMING else N - 1
             waiter(qkv_recv.at[0, pl.ds(0, count)], 1 + plane).wait_send()
-            waiter(tile.at[plane], 3 + plane).wait_send()
+            waiter(tile_out, 3 + plane).wait_send()
 
     @pl.when(jnp.logical_not(sums & (me < OWNERS)))
     def _():
@@ -567,6 +583,7 @@
     @pl.when(sums)
     def _():
         waiter(part_recv.at[0, pl.ds(0, N - 1)], 5).wait_send()
+        waiter(stat_recv.at[0, pl.ds(0, N - 1)], 14).wait_send()
         for plane in range(C):
             count = len(NEAR) + (plane != SUMMING)
             waiter(attn_all.at[pl.ds(0, count)], 6 + plane).wait_send()
@@ -574,6 +591,7 @@
     @pl.when(my_c != SUMMING)
     def _():
         waiter(part_recv.at[0], 5).wait_send()
+        waiter(stat_recv.at[0], 14).wait_send()
 
     waiter(head_recv.at[pl.ds(0, len(HEADS))], 8).wait_send()
     waiter(last_recv.at[pl.ds(0, len(HEADS))], 9).wait_send()
@@ -583,7 +601,7 @@
         waiter(ff_recv.at[0, pl.ds(0, tiles_ff - 1)], 10).wait_send()
         for plane in range(C):
             count = N if plane != SUMMING else N - 1
-            waiter(part_recv.at[0, pl.ds(0, count)], 11 + plane).wait_send()
+            waiter(ff_recv.at[0, pl.ds(0, count), 0], 11 + plane).wait_send()
 
     @pl.when(jnp.logical_not(summing_tile))
     def _():
@@ -637,8 +655,11 @@
             pltpu.VMEM((C, N, REST, D), BF16),
             pltpu.VMEM((B, G, D), BF16),
             pltpu.VMEM((C, 2 * G, D), BF16),
-            pltpu.VMEM((B, 2 * G, D), BF16),
-            pltpu.VMEM((C, N, 2 * G, D), BF16),
+            pltpu.VMEM((C, 2 * G, D), BF16),
+            pltpu.VMEM((B, G, D), BF16),
+            pltpu.VMEM((C, N, G, D), BF16),
+            pltpu.VMEM((B, 1, LANES), F32),
+            pltpu.VMEM((C, N, LANES), F32),
             pltpu.VMEM((C, G, D), BF16),
             pltpu.VMEM((B, G, D), BF16),
             pltpu.VMEM((B * G, D), F32),
@@ -654,11 +675,11 @@
             pltpu.SMEM((N,), jnp.int32),
             pltpu.SemaphoreType.DMA((15,)),
             pltpu.SemaphoreType.DMA((ROWS,)),
-            pltpu.SemaphoreType.DMA((4, C)),
+            pltpu.SemaphoreType.DMA((5, C)),
             pltpu.SemaphoreType.DMA((C,)),
             pltpu.SemaphoreType.DMA((2,)),
-            pltpu.SemaphoreType.DMA((14,)),
-            pltpu.SemaphoreType.DMA((14,)),
+            pltpu.SemaphoreType.DMA((15,)),
+            pltpu.SemaphoreType.DMA((15,)),
         ],
         compiler_params=pltpu.CompilerParams(collective_id=0, has_side_effects=True),
     )(

time: 54 us -> 53.8 us (level)
  no operation moved by 1% of the time
where the time goes in v2:
time: 53.8 us; the launch traced here: 53.6 us
  Pallas kernels  53 us (99%)
  local copies, waits for them, and re-layouts  0.6 us (1%)
    pallas_call x1, Pallas kernels, on_device(): pl.pallas_call(functools.partial(kernel, tiles_ff, ff), out_shape=pltpu.V...  53 us

profile of v2, /device:TPU:1, one launch (start us, length us, event | category | flops | bytes accessed | tf_op | source)
XLA Modules:
  0.0 53.6 jit_solution(14419895585242948196)
XLA Ops:
  0.0 53.0 %shard_map.118 = bf16[16,256]{1,0:T(8,128)(2,1)S(1)} custom-call(bf16[16,256]{1,0:T(8,128)(2,1)} %hidden_hbm.1, bf16[256]{0:T(256)(128)(2,1)} %attn_gain_hbm.1, bf16[256,1280]{1,0:T(8,128)(2,1)} %bitcast.9, bf16[64,128,128]{2,1,0:T(8,128)(2,1)} %bitcast.7, bf16[64,128,128]{2,1,0:T(8,128)(2,1)} %bitcast.8, s32[4,16]{1,0:T(4,128)} %bitcast.11, s32[16]{0:T(128)} %lengths_hbm.1, ...), custom_call_target="tpu_custom_call" | custom-call | tf_op jit(solution)/shard_map/pallas_call | solution.py:631
  53.0 0.6 %copy.14 = bf16[16,256]{1,0:T(8,128)(2,1)} copy(bf16[16,256]{1,0:T(8,128)(2,1)S(1)} %shard_map.118) | data formatting | bytes 16384

commit v3 on v2

--- a/solution.py
+++ b/solution.py
@@ -43,7 +43,10 @@
 
 
 def far_first(offsets, sizes):
-    return sorted(offsets, key=lambda at: -sum(around(o, s) for o, s in zip(at, sizes)))
+    return sorted(
+        offsets,
+        key=lambda at: (-sum(around(o, s) for o, s in zip(at, sizes)), -around(at[0], sizes[0])),
+    )
 
 
 ALL = far_first([(dz, dx) for dz in range(Z) for dx in range(X) if (dz, dx) != (0, 0)], (Z, X))
@@ -327,7 +330,7 @@
     def _():
         qkv_recv[SUMMING, me] = qkv_send[me]
         rest_recv[SUMMING, me] = rest_send[me]
-        for plane in (SUMMING, 1 - SUMMING):
+        for plane in (1 - SUMMING, SUMMING):
             wait_parts(rest_recv, 3, plane)
             rest = jnp.sum(rest_recv[plane].astype(F32), axis=0)
             square = rest[SQUARE_ROW - G : SQUARE_ROW - G + 1]
@@ -443,7 +446,7 @@
     def _():
         part_recv[SUMMING, me] = part_send[my_request]
         stat_recv[SUMMING, pl.ds(me, 1)] = stat_send[my_request]
-        for plane in (SUMMING, 1 - SUMMING):
+        for plane in (1 - SUMMING, SUMMING):
 
             waiter(tile.at[plane], 0, tile_sem.at[plane]).wait_recv()
             known = tile[plane].astype(F32)
@@ -534,7 +537,7 @@
     @pl.when(summing_tile)
     def _():
         ff_recv[SUMMING, me] = ff_send[my_tile]
-        for plane in (SUMMING, 1 - SUMMING):
+        for plane in (1 - SUMMING, SUMMING):
             wait_parts(ff_recv, 2, plane)
             both = jnp.sum(ff_recv[plane].astype(F32), axis=0)
             square = both[0][:, TILE : TILE + 1] + both[0][:, TILE + 1 : TILE + 2]

time: 53.8 us -> 53.2 us (0.989)
  Pallas kernels: 53 us -> 52.4 us
    pallas_call x1, Pallas kernels: 53 us -> 52.4 us  [on_device(): pl.pallas_call(functools.partial(kernel, tiles_ff, ff), out_shape=pltpu.V...]
where the time goes in v3:
time: 53.2 us; the launch traced here: 53 us
  Pallas kernels  52.4 us (98%)
  local copies, waits for them, and re-layouts  0.6 us (1%)
    pallas_call x1, Pallas kernels, on_device(): pl.pallas_call(functools.partial(kernel, tiles_ff, ff), out_shape=pltpu.V...  52.4 us

profile of v3, /device:TPU:1, one launch (start us, length us, event | category | flops | bytes accessed | tf_op | source)
XLA Modules:
  0.0 53.0 jit_solution(12162412689262457959)
XLA Ops:
  0.0 52.4 %shard_map.118 = bf16[16,256]{1,0:T(8,128)(2,1)S(1)} custom-call(bf16[16,256]{1,0:T(8,128)(2,1)} %hidden_hbm.1, bf16[256]{0:T(256)(128)(2,1)} %attn_gain_hbm.1, bf16[256,1280]{1,0:T(8,128)(2,1)} %bitcast.9, bf16[64,128,128]{2,1,0:T(8,128)(2,1)} %bitcast.7, bf16[64,128,128]{2,1,0:T(8,128)(2,1)} %bitcast.8, s32[4,16]{1,0:T(4,128)} %bitcast.11, s32[16]{0:T(128)} %lengths_hbm.1, ...), custom_call_target="tpu_custom_call" | custom-call | tf_op jit(solution)/shard_map/pallas_call | solution.py:634
  52.4 0.6 %copy.14 = bf16[16,256]{1,0:T(8,128)(2,1)} copy(bf16[16,256]{1,0:T(8,128)(2,1)S(1)} %shard_map.118) | data formatting | bytes 16384
